TPU v7x, 32 devices: a whole 2x2x4 slice. The times are simulated.
32 devices in a mesh: atom: 4 (over y, x), tm: 8 (over z, core).
Axes of the slice: x: 2, y: 2, z: 4, core: 2. Of those that a mesh axis runs over, the one named last changes fastest.
Arguments:
- signal: bfloat16 [306, 8192], P(None, 'tm'), may hold values from -6 to 6
- spatial: bfloat16 [256, 306], P('atom'), may hold values from -0.3125 to 0.3125
- temporal: bfloat16 [256, 256], P('atom'), may hold values from -0.375 to 0.375
- code_values: bfloat16 [256, 8192], P('atom', 'tm'), may hold values from 0 to 2
- block_mask: int32 [256, 32], P('atom', 'tm'), may hold values 0 or 1
Outputs:
- grad_spatial: float32 [256, 306], P('atom')
- grad_temporal: float32 [256, 256], P('atom')
All inputs are finite; a program needn't handle non-finite values. No bound on the sum of `block_mask` on one device may be relied on, other than what follows from the above.
Results may differ from a plain program's by a relative error of at most 0.0025.
Values may be sent and summed in bfloat16 or wider, within the bound.
A program may use at most 64 MiB of HBM per device.

v0:
```python
import math

import jax
import jax.numpy as jnp
from jax import lax
from jax.sharding import PartitionSpec as P


def shifted(block, axis, distance):
    devices = range(lax.axis_size(axis))
    route = [(i - distance, i) for i in devices if i - distance in devices]
    return lax.ppermute(block, axis, route)


def toeplitz(kernels):
    count, length = kernels.shape
    heads = jnp.concatenate([jnp.zeros((count, 2 * length), kernels.dtype), kernels], axis=1)
    tiled = jnp.tile(heads, (1, 2 * length))[:, : 2 * length * (3 * length - 1)]
    return tiled.reshape(count, 2 * length, 3 * length - 1)[:, :, :length]


def diagonals(products):
    count, rows_all, length = products.shape
    padded = jnp.concatenate(
        [jnp.zeros((count, rows_all, 2 * length), products.dtype), products], axis=2
    )
    padded = padded.reshape(count, rows_all * 3 * length)
    padded = jnp.concatenate([padded, jnp.zeros((count, rows_all), products.dtype)], axis=1)
    skewed = padded.reshape(count, rows_all, 3 * length + 1)
    return jnp.sum(skewed, axis=1)[:, length : 2 * length]


def windows_of(extended, length):
    count, total = extended.shape
    blocks = extended.reshape(count, total // length, length)
    return jnp.concatenate([blocks[:, :-1], blocks[:, 1:]], axis=2)


def courses_of(extended, kernels, length, samples):
    count = extended.shape[0]

    def forward_group(operands):
        ext_group, group_kernels = operands
        windows = windows_of(ext_group, length)
        matrix = toeplitz(group_kernels)
        course_group = jnp.einsum(
            "gbm,gms->gbs", windows, matrix, preferred_element_type=jnp.float32
        )
        return course_group.reshape(4, samples).astype(jnp.bfloat16)

    result = lax.map(
        forward_group,
        (extended.reshape(count // 4, 4, length + samples), kernels.reshape(count // 4, 4, length)),
    )
    return result.reshape(count, samples)


def local(signal, spatial, temporal, code_values, block_mask):
    atoms, channels = spatial.shape
    length = temporal.shape[1]
    samples = signal.shape[1]
    nblocks = samples // length
    groups = atoms // 4
    codes = (
        code_values.reshape(atoms, nblocks, length) * block_mask[:, :, None].astype(jnp.bfloat16)
    ).reshape(atoms, samples)
    previous = shifted(codes[:, samples - length :], "tm", 1)
    extended = jnp.concatenate([previous, codes], axis=1)
    ext_groups = extended.reshape(groups, 4, length + samples)
    course = courses_of(extended, temporal, length, samples)
    partial_value = jnp.dot(spatial.T, course, preferred_element_type=jnp.float32)
    share = lax.psum_scatter(
        partial_value.astype(jnp.bfloat16), "atom", scatter_dimension=1, tiled=True
    ).astype(jnp.float32)
    width = share.shape[1]
    start = lax.axis_index("atom") * width
    own_signal = lax.dynamic_slice_in_dim(signal, start, width, 1)
    residual_part = (share - own_signal.astype(jnp.float32)).astype(jnp.bfloat16)
    residual = lax.all_gather(residual_part, "atom", axis=1, tiled=True)
    projected = jnp.dot(spatial, residual, preferred_element_type=jnp.float32).astype(jnp.bfloat16)
    spatial_part = lax.dot_general(
        course, residual, (((1,), (1,)), ((), ())), preferred_element_type=jnp.float32
    )

    def adjoint_group(operands):
        ext_group, proj_group = operands
        windows = windows_of(ext_group, length)
        proj_blocks = proj_group.reshape(4, nblocks, length)
        products = jnp.einsum(
            "gbm,gbs->gms", windows, proj_blocks, preferred_element_type=jnp.float32
        )
        return diagonals(products)

    temporal_part = lax.map(
        adjoint_group, (ext_groups, projected.reshape(groups, 4, samples))
    ).reshape(atoms, length)
    spatial_sum, temporal_sum = lax.psum((spatial_part, temporal_part), "tm")
    factor = 1.0 / math.sqrt(samples * lax.axis_size("tm"))
    return (spatial_sum * factor, temporal_sum * factor)


def solution(mesh):
    in_specs = (P(None, "tm"), P("atom", None), P("atom", None), P("atom", "tm"), P("atom", "tm"))
    out_specs = (P("atom", None), P("atom", None))
    return jax.shard_map(local, mesh=mesh, in_specs=in_specs, out_specs=out_specs, check_vma=False)
```

profile of v0, /device:TPU:0, one launch (start us, length us, event | category | flops | bytes accessed | tf_op | source)
XLA Modules:
  0.0 805.1 jit_solution(13150680760445577018)
XLA Ops:
  12.5 252.7 %while.20 = (s32[]{:T(128)}, bf16[16,4,1024]{2,1,0:T(4,128)(2,1)S(1)}, bf16[16,4,1280]{2,1,0:T(4,128)(2,1)S(1)}, bf16[16,4,256]{2,1,0:T(4,128)(2,1)S(1)}, s32[]{:T(128)}, /*index=5*/bf16[]{:T(256)}) while((s32[]{:T(128)}, bf16[16,4,1024]{2,1,0:T(4,128)(2,1)S(1)}, bf16[16,4,1280]{2,1,0:T(4,128)(2,1)S(1)}, bf16[16,4,256]{2,1,0:T(4,128)(2,1)S(1)}, ...), condition=%wide.region_1.2_spmd, body=%wide.region_0.1_spmd.sunk | while | flops 4231170 | bytes 29485140 | solution.py:51
  19.3 8.8 %reshape.75 = bf16[4,512,767]{2,1,0:T(8,128)(2,1)S(1)} reshape(bf16[1570816]{0:T(1024)(128)(2,1)} %reshape.74) | data formatting | bytes 6283264 | tf_op jit(solution)/shard_map/while/body/eval_jaxpr/reshape | solution.py:19
  35.1 8.8 %reshape.75 = bf16[4,512,767]{2,1,0:T(8,128)(2,1)S(1)} reshape(bf16[1570816]{0:T(1024)(128)(2,1)} %reshape.74) | data formatting | bytes 6283264 | tf_op jit(solution)/shard_map/while/body/eval_jaxpr/reshape | solution.py:19
  50.9 8.8 %reshape.75 = bf16[4,512,767]{2,1,0:T(8,128)(2,1)S(1)} reshape(bf16[1570816]{0:T(1024)(128)(2,1)} %reshape.74) | data formatting | bytes 6283264 | tf_op jit(solution)/shard_map/while/body/eval_jaxpr/reshape | solution.py:19
  266.6 30.2 %reduce-scatter.2.cloned.1.call-done = bf16[306,256]{1,0:T(8,128)(2,1)} async-done(((bf16[306,1024]{1,0:T(8,128)(2,1)}), bf16[306,256]{1,0:T(8,128)(2,1)}) %reduce-scatter.2.cloned.1.call-update) | async-done | bytes 156688 | tf_op jit(solution)/shard_map/reduce_scatter | solution.py:72
  297.8 14.9 %all_gather.3 = bf16[306,1024]{1,0:T(8,128)(2,1)S(1)} all-gather(bf16[306,256]{1,0:T(8,128)(2,1)S(1)} %subtract_convert_fusion), channel_id=1, replica_groups=mesh['atom'=4,'tm'=8] {'atom'}, dimensions={1}, use_global_device_ids=true | all-gather | bytes 783360 | tf_op jit(solution)/shard_map/all_gather | solution.py:79
  314.0 427.7 %while.21 = (s32[]{:T(128)}, f32[16,4,256]{2,1,0:T(4,128)S(1)}, bf16[16,4,1280]{2,1,0:T(4,128)(2,1)S(1)}, bf16[16,4,1024]{2,1,0:T(4,128)(2,1)S(1)}, s32[]{:T(128)}, /*index=5*/f32[]{:T(128)}) while((s32[]{:T(128)}, f32[16,4,256]{2,1,0:T(4,128)S(1)}, bf16[16,4,1280]{2,1,0:T(4,128)(2,1)S(1)}, bf16[16,4,1024]{2,1,0:T(4,128)(2,1)S(1)}, s32[]{:T(128)}, ...), condition=%wide.region_6.7_spmd, body=%wide.region_4.6_spmd.sunk | while | flops 5798910 | bytes 54710376 | solution.py:94
  322.9 14.5 %reshape.79 = f32[4,512,769]{2,1,0:T(8,128)} reshape(f32[4,393728]{1,0:T(4,128)} %concatenate.32) | data formatting | bytes 12599296 | tf_op jit(solution)/shard_map/while/body/eval_jaxpr/reshape | solution.py:29
  349.7 14.5 %reshape.79 = f32[4,512,769]{2,1,0:T(8,128)} reshape(f32[4,393728]{1,0:T(4,128)} %concatenate.32) | data formatting | bytes 12599296 | tf_op jit(solution)/shard_map/while/body/eval_jaxpr/reshape | solution.py:29
  376.4 14.5 %reshape.79 = f32[4,512,769]{2,1,0:T(8,128)} reshape(f32[4,393728]{1,0:T(4,128)} %concatenate.32) | data formatting | bytes 12599296 | tf_op jit(solution)/shard_map/while/body/eval_jaxpr/reshape | solution.py:29
  403.1 14.5 %reshape.79 = f32[4,512,769]{2,1,0:T(8,128)} reshape(f32[4,393728]{1,0:T(4,128)} %concatenate.32) | data formatting | bytes 12599296 | tf_op jit(solution)/shard_map/while/body/eval_jaxpr/reshape | solution.py:29
  429.8 14.5 %reshape.79 = f32[4,512,769]{2,1,0:T(8,128)} reshape(f32[4,393728]{1,0:T(4,128)} %concatenate.32) | data formatting | bytes 12599296 | tf_op jit(solution)/shard_map/while/body/eval_jaxpr/reshape | solution.py:29
  456.5 14.5 %reshape.79 = f32[4,512,769]{2,1,0:T(8,128)} reshape(f32[4,393728]{1,0:T(4,128)} %concatenate.32) | data formatting | bytes 12599296 | tf_op jit(solution)/shard_map/while/body/eval_jaxpr/reshape | solution.py:29
  483.3 14.5 %reshape.79 = f32[4,512,769]{2,1,0:T(8,128)} reshape(f32[4,393728]{1,0:T(4,128)} %concatenate.32) | data formatting | bytes 12599296 | tf_op jit(solution)/shard_map/while/body/eval_jaxpr/reshape | solution.py:29
  510.0 14.5 %reshape.79 = f32[4,512,769]{2,1,0:T(8,128)} reshape(f32[4,393728]{1,0:T(4,128)} %concatenate.32) | data formatting | bytes 12599296 | tf_op jit(solution)/shard_map/while/body/eval_jaxpr/reshape | solution.py:29
  536.7 14.5 %reshape.79 = f32[4,512,769]{2,1,0:T(8,128)} reshape(f32[4,393728]{1,0:T(4,128)} %concatenate.32) | data formatting | bytes 12599296 | tf_op jit(solution)/shard_map/while/body/eval_jaxpr/reshape | solution.py:29
  563.4 14.5 %reshape.79 = f32[4,512,769]{2,1,0:T(8,128)} reshape(f32[4,393728]{1,0:T(4,128)} %concatenate.32) | data formatting | bytes 12599296 | tf_op jit(solution)/shard_map/while/body/eval_jaxpr/reshape | solution.py:29
  590.1 14.5 %reshape.79 = f32[4,512,769]{2,1,0:T(8,128)} reshape(f32[4,393728]{1,0:T(4,128)} %concatenate.32) | data formatting | bytes 12599296 | tf_op jit(solution)/shard_map/while/body/eval_jaxpr/reshape | solution.py:29
  616.9 14.5 %reshape.79 = f32[4,512,769]{2,1,0:T(8,128)} reshape(f32[4,393728]{1,0:T(4,128)} %concatenate.32) | data formatting | bytes 12599296 | tf_op jit(solution)/shard_map/while/body/eval_jaxpr/reshape | solution.py:29
  643.6 14.5 %reshape.79 = f32[4,512,769]{2,1,0:T(8,128)} reshape(f32[4,393728]{1,0:T(4,128)} %concatenate.32) | data formatting | bytes 12599296 | tf_op jit(solution)/shard_map/while/body/eval_jaxpr/reshape | solution.py:29
  670.3 14.5 %reshape.79 = f32[4,512,769]{2,1,0:T(8,128)} reshape(f32[4,393728]{1,0:T(4,128)} %concatenate.32) | data formatting | bytes 12599296 | tf_op jit(solution)/shard_map/while/body/eval_jaxpr/reshape | solution.py:29
  697.0 14.5 %reshape.79 = f32[4,512,769]{2,1,0:T(8,128)} reshape(f32[4,393728]{1,0:T(4,128)} %concatenate.32) | data formatting | bytes 12599296 | tf_op jit(solution)/shard_map/while/body/eval_jaxpr/reshape | solution.py:29
  723.7 14.5 %reshape.79 = f32[4,512,769]{2,1,0:T(8,128)} reshape(f32[4,393728]{1,0:T(4,128)} %concatenate.32) | data formatting | bytes 12599296 | tf_op jit(solution)/shard_map/while/body/eval_jaxpr/reshape | solution.py:29
  742.4 52.9 %all-reduce.6.cloned.1.call-done = (f32[64,306]{1,0:T(8,128)}, f32[64,256]{1,0:T(8,128)}) async-done(((f32[64,306]{1,0:T(8,128)}, f32[64,256]{1,0:T(8,128)}), (f32[64,306]{1,0:T(8,128)}, f32[64,256]{1,0:T(8,128)})) %all-reduce.6.cloned.1.call-update) | async-done | bytes 143888 | tf_op jit(solution)/shard_map/psum | solution.py:97
  (411 shorter events, 432.0 us)
Async XLA Ops:
  7.2 258.1 %copy-start = (bf16[64,306]{1,0:T(8,128)(2,1)S(1)}, bf16[64,306]{1,0:T(8,128)(2,1)}, u32[]{:S(2)}) copy-start(bf16[64,306]{1,0:T(8,128)(2,1)} %param.10) | copy-start | bytes 117508
  7.2 289.6 %reduce-scatter.2.cloned.1.call-start = ((), (), s32[]{:S(2)}) async-start(), calls=%async_computation.1 | async-start | bytes 798720 | tf_op jit(solution)/shard_map/reduce_scatter | solution.py:72
  9.2 3.3 collective-permute-start
  266.5 528.8 %all-reduce.6.cloned.1.call-start = ((), (), s32[]{:S(2)}) async-start(), calls=%async_computation.2 | async-start | bytes 327680 | tf_op jit(solution)/shard_map/psum | solution.py:97
Sparse Core Ops, SparseCore 0:
  266.6 30.0 reduce-scatter.1
  742.5 52.6 all-reduce.5
where the time goes:
time: 807 us; the launch traced here: 805 us
  local copies, waits for them, and re-layouts  613 us (76%)
  waiting for transfers between devices  83.1 us (10%)
  other arithmetic  61 us (8%)
  blocking collectives  14.9 us (2%)
  between operations  14.2 us (2%)
  matrix products  14.1 us (2%)
    reshape x16, local copies, waits for them, and re-layouts, diagonals(): skewed = padded.reshape(count, rows_all, 3 * length + 1)  232 us
    while x80, local copies, waits for them, and re-layouts  161 us
    reshape x16, local copies, waits for them, and re-layouts, toeplitz(): return tiled.reshape(count, 2 * length, 3 * length - 1)[:, :, :length]  140 us
    concatenate x16, local copies, waits for them, and re-layouts, diagonals(): jnp.concatenate([padded, jnp.zeros((count, rows_all), products.dtype)], a...  56.9 us
    reduce_sum x16, other arithmetic, diagonals(): return jnp.sum(skewed, axis=1)[:, length:2 * length]  55.3 us
    psum x1, waiting for transfers between devices, local(): spatial_sum, temporal_sum = lax.psum((spatial_part, temporal_part), 'tm')  52.9 us
    reduce_scatter x1, waiting for transfers between devices, local(): lax.psum_scatter(partial_value.astype(jnp.bfloat16), 'atom', scatter_dime...  30.2 us
    slice x16, local copies, waits for them, and re-layouts, toeplitz(): tiled = jnp.tile(heads, (1, 2 * length))[:, :2 * length * (3 * length - 1)]  18.4 us
  transfers between devices with their start and end apart: 3, of which 2 were waited for; matrix products, arithmetic and copies ran while one was open for 0% of the time, Pallas kernels for 0%

commit v1 on v0

v1 whole, which is shorter than its diff:
```python
import functools
import math

import jax
import jax.numpy as jnp
from jax import lax
from jax.experimental import pallas as pl
from jax.experimental.pallas import tpu as pltpu
from jax.sharding import PartitionSpec as P

LANES = 128
ROWS = 128
MESH = pl.DeviceIdType.MESH
F32 = jnp.float32
BF16 = jnp.bfloat16


def kernel(
    n_atom, n_tm, factor,
    signal_ref, spatial_ref, temporal_ref, values_ref, mask_ref,
    out_sp_ref, out_tm_ref,
    tail, halo, x, w, cbuf, ctbuf, sbuf, weights, own_w, sig, sig_t, proj, taps,
    sp_part, sp_recv, sp_full, tm_part, tm_recv, tm_full,
    halo_sems, s_send, s_recv, c_send, c_recv,
    sp_send, sp_rsem, sp_gsend, sp_grecv, tm_send, tm_rsem, tm_gsend, tm_grecv,
):
    atoms, channels = spatial_ref.shape
    length = temporal_ref.shape[1]
    samples = signal_ref.shape[1]
    blocks = mask_ref.shape[1]
    block = samples // blocks
    fold = LANES // atoms
    seg = samples // fold
    chunks = seg // ROWS
    share = atoms // n_tm
    me_a = lax.axis_index("atom")
    me_t = lax.axis_index("tm")
    a_peers = [lax.rem(me_a + d, n_atom) for d in range(1, n_atom)]
    t_peers = [lax.rem(me_t + d, n_tm) for d in range(1, n_tm)]

    barrier = pltpu.get_barrier_semaphore()
    for peer in a_peers:
        pl.semaphore_signal(barrier, inc=1, device_id={"atom": peer}, device_id_type=MESH)
    for peer in t_peers:
        pl.semaphore_signal(barrier, inc=1, device_id={"tm": peer}, device_id_type=MESH)

    mask = mask_ref[...].astype(F32)
    codes = jnp.concatenate(
        [
            values_ref[:, j * block : (j + 1) * block].astype(F32) * mask[:, j : j + 1]
            for j in range(blocks)
        ],
        axis=1,
    )
    tail[...] = codes[:, samples - length :].astype(BF16)

    pl.semaphore_wait(barrier, n_atom - 1 + n_tm - 1)

    right = lax.rem(me_t + 1, n_tm)
    halo_copy = pltpu.make_async_remote_copy(
        src_ref=tail, dst_ref=halo, send_sem=halo_sems.at[0], recv_sem=halo_sems.at[1],
        device_id={"tm": right}, device_id_type=MESH,
    )

    @pl.when(me_t < n_tm - 1)
    def _():
        halo_copy.start()

    s_copies = []
    for d, peer in enumerate(a_peers):
        copy = pltpu.make_async_remote_copy(
            src_ref=spatial_ref, dst_ref=sbuf.at[me_a], send_sem=s_send.at[d],
            recv_sem=s_recv.at[d], device_id={"atom": peer}, device_id_type=MESH,
        )
        copy.start()
        s_copies.append(copy)

    stacked = jnp.concatenate([codes[:, h * seg : (h + 1) * seg] for h in range(fold)], axis=0)
    x[length:, :] = stacked.T
    w[...] = jnp.concatenate([temporal_ref[...].astype(F32)] * fold, axis=0).T

    c_copies = [[None] * (n_atom - 1) for _ in range(chunks)]

    def convolve(c):
        base = length + c * ROWS

        def body(a, acc):
            for b in range(8):
                start = pl.multiple_of(base - 24 - 32 * a, 8) - b
                xs = x[pl.ds(start, ROWS + 24), :]
                for q in range(4):
                    tap = w[pl.ds(32 * a + 8 * q + b, 1), :]
                    acc = acc + xs[24 - 8 * q : 24 - 8 * q + ROWS] * tap
            return acc

        acc = lax.fori_loop(0, length // 32, body, jnp.zeros((ROWS, LANES), F32))
        course = acc.astype(BF16)
        rows = pl.ds(c * ROWS, ROWS)
        cbuf[me_a, rows, :] = course
        for d, peer in enumerate(a_peers):
            copy = pltpu.make_async_remote_copy(
                src_ref=cbuf.at[me_a, rows], dst_ref=cbuf.at[me_a, rows],
                send_sem=c_send.at[d, c], recv_sem=c_recv.at[d, c],
                device_id={"atom": peer}, device_id_type=MESH,
            )
            copy.start()
            c_copies[c][d] = copy
        ctbuf[c] = course.astype(F32).T.astype(BF16)

    late = [c for c in range(chunks) if c * ROWS >= length]
    early = [c for c in range(chunks) if c * ROWS < length]
    for c in late:
        convolve(c)

    @pl.when(me_t == 0)
    def _():
        halo[...] = jnp.zeros(halo.shape, halo.dtype)

    @pl.when(me_t > 0)
    def _():
        halo_copy.wait_recv()

    before = jnp.concatenate(
        [halo[...].astype(F32)] + [codes[:, h * seg - length : h * seg] for h in range(1, fold)],
        axis=0,
    )
    x[:length, :] = before.T
    for c in early:
        convolve(c)

    padded = sig.shape[0]
    sig[channels // 8 * 8 :, :] = jnp.zeros((padded - channels // 8 * 8, samples), F32)
    sig[:channels, :] = signal_ref[...].astype(F32)
    for c in range(samples // ROWS):
        sig_t[c * ROWS : (c + 1) * ROWS, :] = sig[:, c * ROWS : (c + 1) * ROWS].T

    sbuf[me_a] = spatial_ref[...]
    for copy in s_copies:
        copy.wait_recv()
    weights[...] = jnp.zeros(weights.shape, BF16)
    own_w[...] = jnp.zeros(own_w.shape, BF16)
    for h in range(fold):
        for g in range(n_atom):
            weights[h, g * LANES + h * atoms : g * LANES + (h + 1) * atoms, :channels] = sbuf[g]
        own_w[h, h * atoms : (h + 1) * atoms, :channels] = spatial_ref[...]

    gsp = None
    for c in late + early:
        for copy in c_copies[c]:
            copy.wait_recv()
        rows = slice(c * ROWS, (c + 1) * ROWS)
        lhs = jnp.concatenate([cbuf[g, rows, :] for g in range(n_atom)], axis=1)
        projected = None
        for h in range(fold):
            model = jnp.dot(lhs, weights[h], preferred_element_type=F32)
            at = h * seg + c * ROWS
            residual = (model - sig_t[at : at + ROWS, :]).astype(BF16)
            part = lax.dot_general(
                residual, own_w[h], (((1,), (1,)), ((), ())), preferred_element_type=F32
            )
            projected = part if projected is None else projected + part
            grad = jnp.dot(
                ctbuf[c, h * atoms : (h + 1) * atoms, :], residual, preferred_element_type=F32
            )
            gsp = grad if gsp is None else gsp + grad
        proj[rows, :] = projected.astype(BF16).astype(F32)

    def scatter(part, recv, send_sems, recv_sems):
        copies = []
        for d, peer in enumerate(t_peers):
            copy = pltpu.make_async_remote_copy(
                src_ref=part.at[peer], dst_ref=recv.at[d], send_sem=send_sems.at[d],
                recv_sem=recv_sems.at[d], device_id={"tm": peer}, device_id_type=MESH,
            )
            copy.start()
            copies.append(copy)
        return copies

    def gather(part, recv, full, copies, send_sems, recv_sems):
        total = part[me_t]
        for d, copy in enumerate(copies):
            copy.wait_recv()
            total = total + recv[d]
        full[me_t] = total * factor
        sent = []
        for d, peer in enumerate(t_peers):
            copy = pltpu.make_async_remote_copy(
                src_ref=full.at[me_t], dst_ref=full.at[me_t], send_sem=send_sems.at[d],
                recv_sem=recv_sems.at[d], device_id={"tm": peer}, device_id_type=MESH,
            )
            copy.start()
            sent.append(copy)
        return sent

    for j in range(n_tm):
        sp_part[j] = gsp[j * share : (j + 1) * share, :]
    sp_copies = scatter(sp_part, sp_recv, sp_send, sp_rsem)

    def correlate(lo, hi):
        def body(a, carry):
            for b in range(8):
                accs = [None] * 8
                for c in range(chunks):
                    p = proj[c * ROWS : (c + 1) * ROWS, :]
                    start = pl.multiple_of(length + c * ROWS - 56 - 64 * a, 8) - b
                    xs = x[pl.ds(start, ROWS + 56), :]
                    for q in range(8):
                        piece = p * xs[56 - 8 * q : 56 - 8 * q + ROWS]
                        for i in range(ROWS // 8):
                            row = piece[8 * i : 8 * i + 8]
                            accs[q] = row if accs[q] is None else accs[q] + row
                for q in range(8):
                    taps[pl.ds(64 * a + 8 * q + b, 1), :] = jnp.sum(accs[q], axis=0, keepdims=True)
            return carry

        lax.fori_loop(lo, hi, body, 0)

    halves = tm_part.shape[0]
    width = length // halves
    tm_copies = []
    sp_sent = None
    for half in range(halves):
        correlate(half * width // 64, (half + 1) * width // 64)
        if half == 0:
            sp_sent = gather(sp_part, sp_recv, sp_full, sp_copies, sp_gsend, sp_grecv)
        spread = taps[half * width : (half + 1) * width, :].T
        gtm = spread[:atoms]
        for h in range(1, fold):
            gtm = gtm + spread[h * atoms : (h + 1) * atoms]
        for j in range(n_tm):
            tm_part[half, j] = gtm[j * share : (j + 1) * share, :]
        tm_copies.append(
            scatter(tm_part.at[half], tm_recv.at[half], tm_send.at[half], tm_rsem.at[half])
        )
    tm_sent = []
    for half in range(halves):
        tm_sent.append(
            gather(
                tm_part.at[half], tm_recv.at[half], tm_full.at[half], tm_copies[half],
                tm_gsend.at[half], tm_grecv.at[half],
            )
        )

    for copy in sp_sent:
        copy.wait_recv()
    for j in range(n_tm):
        out_sp_ref[j * share : (j + 1) * share, :] = sp_full[j][:, :channels]
    for half in range(halves):
        for copy in tm_sent[half]:
            copy.wait_recv()
        for j in range(n_tm):
            out_tm_ref[j * share : (j + 1) * share, half * width : (half + 1) * width] = tm_full[half, j]

    @pl.when(me_t < n_tm - 1)
    def _():
        halo_copy.wait_send()

    for copy in s_copies + [copy for row in c_copies for copy in row]:
        copy.wait_send()
    for copy in sp_copies + sp_sent:
        copy.wait_send()
    for row in tm_copies + tm_sent:
        for copy in row:
            copy.wait_send()


def local(n_atom, n_tm, signal, spatial, temporal, values, mask):
    atoms, channels = spatial.shape
    length = temporal.shape[1]
    samples = signal.shape[1]
    fold = LANES // atoms
    seg = samples // fold
    chunks = seg // ROWS
    share = atoms // n_tm
    wide = -(-channels // LANES) * LANES
    halves = 2
    width = length // halves
    factor = 1.0 / math.sqrt(samples * n_tm)
    dma = pltpu.SemaphoreType.DMA
    vmem = pl.BlockSpec(memory_space=pltpu.VMEM)
    return pl.pallas_call(
        functools.partial(kernel, n_atom, n_tm, factor),
        out_shape=(
            jax.ShapeDtypeStruct((atoms, channels), F32),
            jax.ShapeDtypeStruct((atoms, length), F32),
        ),
        in_specs=[vmem] * 5,
        out_specs=(vmem, vmem),
        scratch_shapes=[
            pltpu.VMEM((atoms, length), BF16),
            pltpu.VMEM((atoms, length), BF16),
            pltpu.VMEM((length + seg, LANES), F32),
            pltpu.VMEM((length, LANES), F32),
            pltpu.VMEM((n_atom, seg, LANES), BF16),
            pltpu.VMEM((chunks, LANES, ROWS), BF16),
            pltpu.VMEM((n_atom, atoms, channels), BF16),
            pltpu.VMEM((fold, n_atom * LANES, wide), BF16),
            pltpu.VMEM((fold, LANES, wide), BF16),
            pltpu.VMEM((wide, samples), F32),
            pltpu.VMEM((samples, wide), F32),
            pltpu.VMEM((seg, LANES), F32),
            pltpu.VMEM((length, LANES), F32),
            pltpu.VMEM((n_tm, share, wide), F32),
            pltpu.VMEM((n_tm - 1, share, wide), F32),
            pltpu.VMEM((n_tm, share, wide), F32),
            pltpu.VMEM((halves, n_tm, share, width), F32),
            pltpu.VMEM((halves, n_tm - 1, share, width), F32),
            pltpu.VMEM((halves, n_tm, share, width), F32),
            dma((2,)),
            dma((n_atom - 1,)),
            dma((n_atom - 1,)),
            dma((n_atom - 1, chunks)),
            dma((n_atom - 1, chunks)),
            dma((n_tm - 1,)),
            dma((n_tm - 1,)),
            dma((n_tm - 1,)),
            dma((n_tm - 1,)),
            dma((halves, n_tm - 1)),
            dma((halves, n_tm - 1)),
            dma((halves, n_tm - 1)),
            dma((halves, n_tm - 1)),
        ],
        compiler_params=pltpu.CompilerParams(collective_id=0, has_side_effects=True),
    )(signal, spatial, temporal, values, mask)


def solution(mesh):
    in_specs = (P(None, "tm"), P("atom", None), P("atom", None), P("atom", "tm"), P("atom", "tm"))
    out_specs = (P("atom", None), P("atom", None))
    body = functools.partial(local, mesh.shape["atom"], mesh.shape["tm"])
    return jax.shard_map(body, mesh=mesh, in_specs=in_specs, out_specs=out_specs, check_vma=False)
```

time: 807 us -> 38.1 us (0.05)
  local copies, waits for them, and re-layouts: 613 us -> 3.59 us
  waiting for transfers between devices: 83.1 us -> 0 us
  other arithmetic: 61 us -> 0 us
  Pallas kernels: 0 us -> 33.6 us
  blocking collectives: 14.9 us -> 0 us
  matrix products: 14.1 us -> 0 us
  between operations: 14.2 us -> 0.65 us
    reshape x84 -> x0, local copies, waits for them, and re-layouts: 374 us -> none  [the longest x16 232 us: diagonals(): skewed = padded.reshape(count, rows_all, 3 * length + 1)]
    while x80 -> x0, local copies, waits for them, and re-layouts: 161 us -> none
    concatenate x35 -> x0, local copies, waits for them, and re-layouts: 57.2 us -> none  [the longest x16 56.9 us: diagonals(): jnp.concatenate([padded, jnp.zeros((count, rows_all), products.dtype)], a...]
    reduce_sum x16 -> x0, other arithmetic: 55.3 us -> none  [diagonals(): return jnp.sum(skewed, axis=1)[:, length:2 * length]]
    psum x1 -> x0, waiting for transfers between devices: 52.9 us -> none  [local(): spatial_sum, temporal_sum = lax.psum((spatial_part, temporal_part), 'tm')]
    pallas_call x0 -> x1, Pallas kernels: none -> 33.6 us  [local(): pl.pallas_call(functools.partial(kernel, n_atom, n_tm, factor), out_shape...]
    reduce_scatter x1 -> x0, waiting for transfers between devices: 30.2 us -> none  [local(): lax.psum_scatter(partial_value.astype(jnp.bfloat16), 'atom', scatter_dime...]
    slice x49 -> x0, local copies, waits for them, and re-layouts: 18.8 us -> none  [the longest x16 18.4 us: toeplitz(): tiled = jnp.tile(heads, (1, 2 * length))[:, :2 * length * (3 * length - 1)]]
  transfers between devices with their start and end apart: 3 -> 0, of which waited for: 2 -> 0; matrix products, arithmetic and copies ran while one was open for 0% -> 0% of each run, Pallas kernels for 0% -> 0%
where the time goes in v1:
time: 38.1 us; the launch traced here: 37.9 us
  Pallas kernels  33.6 us (88%)
  local copies, waits for them, and re-layouts  3.59 us (9%)
  between operations  0.65 us (2%)
    pallas_call x1, Pallas kernels, local(): pl.pallas_call(functools.partial(kernel, n_atom, n_tm, factor), out_shape...  33.6 us
    unnamed x5, local copies, waits for them, and re-layouts  3.59 us

profile of v1, /device:TPU:0, one launch (start us, length us, event | category | flops | bytes accessed | tf_op | source)
XLA Modules:
  0.0 37.9 jit_solution(2709442957761408282)
XLA Ops:
  0.6 1.4 %copy.7.mask_ref = s32[64,4]{1,0:T(8,128)} copy(s32[64,4]{0,1:T(4,128)} %param.9) | data formatting | bytes 2048 | tf_op args[4]
  2.0 33.6 %shard_map.68 = (f32[64,306]{1,0:T(8,128)}, f32[64,256]{1,0:T(8,128)}) custom-call(bf16[306,1024]{1,0:T(8,128)(2,1)} %signal_ref.1, bf16[64,306]{1,0:T(8,128)(2,1)} %spatial_ref.1, bf16[64,256]{1,0:T(8,128)(2,1)} %temporal_ref.1, bf16[64,1024]{1,0:T(8,128)(2,1)} %values_ref.1, s32[64,4]{1,0:T(8,128)} %copy.7.mask_ref), custom_call_target="tpu_custom_call" | custom-call | tf_op jit(solution)/shard_map/pallas_call | solution.py:281
  35.7 0.0 copy-start
  35.7 1.6 %copy.10 = f32[64,306]{1,0:T(8,128)} copy(f32[64,306]{1,0:T(8,128)} %get-tuple-element.4) | data formatting | bytes 156672
  37.2 0.0 copy-done
  37.2 0.6 %copy.11 = f32[64,256]{1,0:T(8,128)} copy(f32[64,256]{1,0:T(8,128)S(1)} %copy-done) | data formatting | bytes 131072
Async XLA Ops:
  35.7 1.6 %copy-start = (f32[64,256]{1,0:T(8,128)S(1)}, f32[64,256]{1,0:T(8,128)}, u32[]{:S(2)}) copy-start(f32[64,256]{1,0:T(8,128)} %get-tuple-element.5) | copy-start | bytes 196612

commit v2 on v1

--- a/solution.py
+++ b/solution.py
@@ -19,7 +19,7 @@
     n_atom, n_tm, factor,
     signal_ref, spatial_ref, temporal_ref, values_ref, mask_ref,
     out_sp_ref, out_tm_ref,
-    tail, halo, x, w, cbuf, ctbuf, sbuf, weights, own_w, sig, sig_t, proj, taps,
+    tail, halo, x, w, cbuf, ctbuf, sbuf, weights, own_w, sig, sig_t, proj, sums, taps,
     sp_part, sp_recv, sp_full, tm_part, tm_recv, tm_full,
     halo_sems, s_send, s_recv, c_send, c_recv,
     sp_send, sp_rsem, sp_gsend, sp_grecv, tm_send, tm_rsem, tm_gsend, tm_grecv,
@@ -27,7 +27,7 @@
     atoms, channels = spatial_ref.shape
     length = temporal_ref.shape[1]
     samples = signal_ref.shape[1]
-    blocks = mask_ref.shape[1]
+    blocks = mask_ref.shape[0]
     block = samples // blocks
     fold = LANES // atoms
     seg = samples // fold
@@ -44,7 +44,7 @@
     for peer in t_peers:
         pl.semaphore_signal(barrier, inc=1, device_id={"tm": peer}, device_id_type=MESH)
 
-    mask = mask_ref[...].astype(F32)
+    mask = mask_ref[...].astype(F32).T
     codes = jnp.concatenate(
         [
             values_ref[:, j * block : (j + 1) * block].astype(F32) * mask[:, j : j + 1]
@@ -54,26 +54,27 @@
     )
     tail[...] = codes[:, samples - length :].astype(BF16)
 
-    pl.semaphore_wait(barrier, n_atom - 1 + n_tm - 1)
-
-    right = lax.rem(me_t + 1, n_tm)
-    halo_copy = pltpu.make_async_remote_copy(
-        src_ref=tail, dst_ref=halo, send_sem=halo_sems.at[0], recv_sem=halo_sems.at[1],
-        device_id={"tm": right}, device_id_type=MESH,
-    )
-
-    @pl.when(me_t < n_tm - 1)
-    def _():
-        halo_copy.start()
-
-    s_copies = []
-    for d, peer in enumerate(a_peers):
-        copy = pltpu.make_async_remote_copy(
-            src_ref=spatial_ref, dst_ref=sbuf.at[me_a], send_sem=s_send.at[d],
-            recv_sem=s_recv.at[d], device_id={"atom": peer}, device_id_type=MESH,
+    def enter():
+
+        right = lax.rem(me_t + 1, n_tm)
+        halo_copy = pltpu.make_async_remote_copy(
+            src_ref=tail, dst_ref=halo, send_sem=halo_sems.at[0], recv_sem=halo_sems.at[1],
+            device_id={"tm": right}, device_id_type=MESH,
         )
-        copy.start()
-        s_copies.append(copy)
+
+        @pl.when(me_t < n_tm - 1)
+        def _():
+            halo_copy.start()
+
+        s_copies = []
+        for d, peer in enumerate(a_peers):
+            copy = pltpu.make_async_remote_copy(
+                src_ref=spatial_ref, dst_ref=sbuf.at[me_a], send_sem=s_send.at[d],
+                recv_sem=s_recv.at[d], device_id={"atom": peer}, device_id_type=MESH,
+            )
+            copy.start()
+            s_copies.append(copy)
+        return halo_copy, s_copies
 
     stacked = jnp.concatenate([codes[:, h * seg : (h + 1) * seg] for h in range(fold)], axis=0)
     x[length:, :] = stacked.T
@@ -97,6 +98,10 @@
         course = acc.astype(BF16)
         rows = pl.ds(c * ROWS, ROWS)
         cbuf[me_a, rows, :] = course
+        ctbuf[c] = course.astype(F32).T.astype(BF16)
+
+    def send(c):
+        rows = pl.ds(c * ROWS, ROWS)
         for d, peer in enumerate(a_peers):
             copy = pltpu.make_async_remote_copy(
                 src_ref=cbuf.at[me_a, rows], dst_ref=cbuf.at[me_a, rows],
@@ -105,12 +110,24 @@
             )
             copy.start()
             c_copies[c][d] = copy
-        ctbuf[c] = course.astype(F32).T.astype(BF16)
 
     late = [c for c in range(chunks) if c * ROWS >= length]
     early = [c for c in range(chunks) if c * ROWS < length]
-    for c in late:
+    if not late:
+        pl.semaphore_wait(barrier, n_atom - 1 + n_tm - 1)
+        halo_copy, s_copies = enter()
+    for i, c in enumerate(late):
         convolve(c)
+        if i == 0:
+            pl.semaphore_wait(barrier, n_atom - 1 + n_tm - 1)
+            halo_copy, s_copies = enter()
+        send(c)
+
+    padded = sig.shape[0]
+    sig[channels // 8 * 8 :, :] = jnp.zeros((padded - channels // 8 * 8, samples), F32)
+    sig[:channels, :] = signal_ref[...].astype(F32)
+    for c in range(samples // ROWS):
+        sig_t[c * ROWS : (c + 1) * ROWS, :] = sig[:, c * ROWS : (c + 1) * ROWS].T
 
     @pl.when(me_t == 0)
     def _():
@@ -127,12 +144,7 @@
     x[:length, :] = before.T
     for c in early:
         convolve(c)
-
-    padded = sig.shape[0]
-    sig[channels // 8 * 8 :, :] = jnp.zeros((padded - channels // 8 * 8, samples), F32)
-    sig[:channels, :] = signal_ref[...].astype(F32)
-    for c in range(samples // ROWS):
-        sig_t[c * ROWS : (c + 1) * ROWS, :] = sig[:, c * ROWS : (c + 1) * ROWS].T
+        send(c)
 
     sbuf[me_a] = spatial_ref[...]
     for copy in s_copies:
@@ -144,8 +156,7 @@
             weights[h, g * LANES + h * atoms : g * LANES + (h + 1) * atoms, :channels] = sbuf[g]
         own_w[h, h * atoms : (h + 1) * atoms, :channels] = spatial_ref[...]
 
-    gsp = None
-    for c in late + early:
+    def process(c, gsp):
         for copy in c_copies[c]:
             copy.wait_recv()
         rows = slice(c * ROWS, (c + 1) * ROWS)
@@ -164,6 +175,7 @@
             )
             gsp = grad if gsp is None else gsp + grad
         proj[rows, :] = projected.astype(BF16).astype(F32)
+        return gsp
 
     def scatter(part, recv, send_sems, recv_sems):
         copies = []
@@ -192,37 +204,47 @@
             sent.append(copy)
         return sent
 
+    def correlate(c, lo, hi, first, last):
+        def body(a, carry):
+            p = proj[c * ROWS : (c + 1) * ROWS, :]
+            for b in range(8):
+                start = pl.multiple_of(length + c * ROWS - 56 - 64 * a, 8) - b
+                xs = x[pl.ds(start, ROWS + 56), :]
+                for q in range(8):
+                    slot = pl.ds(pl.multiple_of(((a * 8 + b) * 8 + q) * 8, 8), 8)
+                    acc = None if first else sums[slot, :]
+                    piece = p * xs[56 - 8 * q : 56 - 8 * q + ROWS]
+                    for i in range(ROWS // 8):
+                        row = piece[8 * i : 8 * i + 8]
+                        acc = row if acc is None else acc + row
+                    if last:
+                        tau = pl.ds(64 * a + 8 * q + b, 1)
+                        taps[tau, :] = jnp.sum(acc, axis=0, keepdims=True)
+                    else:
+                        sums[slot, :] = acc
+            return carry
+
+        lax.fori_loop(lo, hi, body, 0)
+
+    halves = tm_part.shape[0]
+    width = length // halves
+    steps = length // 64
+    order = late + early
+    near = order[: chunks // 2]
+    gsp = None
+    for c in near:
+        gsp = process(c, gsp)
+        correlate(c, 0, steps, c == order[0], False)
+    for c in order[chunks // 2 :]:
+        gsp = process(c, gsp)
     for j in range(n_tm):
         sp_part[j] = gsp[j * share : (j + 1) * share, :]
     sp_copies = scatter(sp_part, sp_recv, sp_send, sp_rsem)
-
-    def correlate(lo, hi):
-        def body(a, carry):
-            for b in range(8):
-                accs = [None] * 8
-                for c in range(chunks):
-                    p = proj[c * ROWS : (c + 1) * ROWS, :]
-                    start = pl.multiple_of(length + c * ROWS - 56 - 64 * a, 8) - b
-                    xs = x[pl.ds(start, ROWS + 56), :]
-                    for q in range(8):
-                        piece = p * xs[56 - 8 * q : 56 - 8 * q + ROWS]
-                        for i in range(ROWS // 8):
-                            row = piece[8 * i : 8 * i + 8]
-                            accs[q] = row if accs[q] is None else accs[q] + row
-                for q in range(8):
-                    taps[pl.ds(64 * a + 8 * q + b, 1), :] = jnp.sum(accs[q], axis=0, keepdims=True)
-            return carry
-
-        lax.fori_loop(lo, hi, body, 0)
-
-    halves = tm_part.shape[0]
-    width = length // halves
+    for c in order[chunks // 2 : -1]:
+        correlate(c, 0, steps, c == order[0], False)
     tm_copies = []
-    sp_sent = None
     for half in range(halves):
-        correlate(half * width // 64, (half + 1) * width // 64)
-        if half == 0:
-            sp_sent = gather(sp_part, sp_recv, sp_full, sp_copies, sp_gsend, sp_grecv)
+        correlate(order[-1], half * width // 64, (half + 1) * width // 64, False, True)
         spread = taps[half * width : (half + 1) * width, :].T
         gtm = spread[:atoms]
         for h in range(1, fold):
@@ -232,6 +254,8 @@
         tm_copies.append(
             scatter(tm_part.at[half], tm_recv.at[half], tm_send.at[half], tm_rsem.at[half])
         )
+        if half == 0:
+            sp_sent = gather(sp_part, sp_recv, sp_full, sp_copies, sp_gsend, sp_grecv)
     tm_sent = []
     for half in range(halves):
         tm_sent.append(
@@ -281,8 +305,8 @@
     return pl.pallas_call(
         functools.partial(kernel, n_atom, n_tm, factor),
         out_shape=(
-            jax.ShapeDtypeStruct((atoms, channels), F32),
-            jax.ShapeDtypeStruct((atoms, length), F32),
+            pltpu.VMEM((atoms, channels), F32),
+            pltpu.VMEM((atoms, length), F32),
         ),
         in_specs=[vmem] * 5,
         out_specs=(vmem, vmem),
@@ -299,6 +323,7 @@
             pltpu.VMEM((wide, samples), F32),
             pltpu.VMEM((samples, wide), F32),
             pltpu.VMEM((seg, LANES), F32),
+            pltpu.VMEM((8 * length, LANES), F32),
             pltpu.VMEM((length, LANES), F32),
             pltpu.VMEM((n_tm, share, wide), F32),
             pltpu.VMEM((n_tm - 1, share, wide), F32),
@@ -321,7 +346,7 @@
             dma((halves, n_tm - 1)),
         ],
         compiler_params=pltpu.CompilerParams(collective_id=0, has_side_effects=True),
-    )(signal, spatial, temporal, values, mask)
+    )(signal, spatial, temporal, values, mask.T)
 
 
 def solution(mesh):

time: 38.1 us -> 33.5 us (0.88)
  local copies, waits for them, and re-layouts: 3.59 us -> 1.27 us
  Pallas kernels: 33.6 us -> 31.5 us
    unnamed x5 -> x2, local copies, waits for them, and re-layouts: 3.59 us -> 1.27 us
    pallas_call x1, Pallas kernels: 33.6 us -> 31.5 us  [local(): pl.pallas_call(functools.partial(kernel, n_atom, n_tm, factor), out_shape...]
where the time goes in v2:
time: 33.5 us; the launch traced here: 33.4 us
  Pallas kernels  31.5 us (94%)
  local copies, waits for them, and re-layouts  1.27 us (4%)
  between operations  0.64 us (2%)
    pallas_call x1, Pallas kernels, local(): pl.pallas_call(functools.partial(kernel, n_atom, n_tm, factor), out_shape...  31.5 us
    unnamed x2, local copies, waits for them, and re-layouts  1.27 us

profile of v2, /device:TPU:0, one launch (start us, length us, event | category | flops | bytes accessed | tf_op | source)
XLA Modules:
  0.0 33.4 jit_solution(17488315802409207686)
XLA Ops:
  0.6 31.5 %shard_map.68 = (f32[64,306]{1,0:T(8,128)S(1)}, f32[64,256]{1,0:T(8,128)S(1)}) custom-call(bf16[306,1024]{1,0:T(8,128)(2,1)} %signal_ref.1, bf16[64,306]{1,0:T(8,128)(2,1)} %spatial_ref.1, bf16[64,256]{1,0:T(8,128)(2,1)} %temporal_ref.1, bf16[64,1024]{1,0:T(8,128)(2,1)} %values_ref.1, s32[4,64]{1,0:T(4,128)} %bitcast.1), custom_call_target="tpu_custom_call" | custom-call | tf_op jit(solution)/shard_map/pallas_call | solution.py:305
  32.1 0.6 %copy.9 = f32[64,306]{1,0:T(8,128)} copy(f32[64,306]{1,0:T(8,128)S(1)} %get-tuple-element.2) | data formatting | bytes 156672
  32.7 0.6 %copy.10 = f32[64,256]{1,0:T(8,128)} copy(f32[64,256]{1,0:T(8,128)S(1)} %get-tuple-element.3) | data formatting | bytes 131072

commit v3 on v2

--- a/solution.py
+++ b/solution.py
@@ -297,7 +297,7 @@
     chunks = seg // ROWS
     share = atoms // n_tm
     wide = -(-channels // LANES) * LANES
-    halves = 2
+    halves = 1
     width = length // halves
     factor = 1.0 / math.sqrt(samples * n_tm)
     dma = pltpu.SemaphoreType.DMA

time: 33.5 us -> 31.3 us (0.934)
  Pallas kernels: 31.5 us -> 29.3 us
    pallas_call x1, Pallas kernels: 31.5 us -> 29.3 us  [local(): pl.pallas_call(functools.partial(kernel, n_atom, n_tm, factor), out_shape...]
where the time goes in v3:
time: 31.3 us; the launch traced here: 31.2 us
  Pallas kernels  29.3 us (94%)
  local copies, waits for them, and re-layouts  1.27 us (4%)
  between operations  0.64 us (2%)
    pallas_call x1, Pallas kernels, local(): pl.pallas_call(functools.partial(kernel, n_atom, n_tm, factor), out_shape...  29.3 us
    unnamed x2, local copies, waits for them, and re-layouts  1.27 us

profile of v3, /device:TPU:0, one launch (start us, length us, event | category | flops | bytes accessed | tf_op | source)
XLA Modules:
  0.0 31.2 jit_solution(2961085919750777347)
XLA Ops:
  0.6 29.3 %shard_map.68 = (f32[64,306]{1,0:T(8,128)S(1)}, f32[64,256]{1,0:T(8,128)S(1)}) custom-call(bf16[306,1024]{1,0:T(8,128)(2,1)} %signal_ref.1, bf16[64,306]{1,0:T(8,128)(2,1)} %spatial_ref.1, bf16[64,256]{1,0:T(8,128)(2,1)} %temporal_ref.1, bf16[64,1024]{1,0:T(8,128)(2,1)} %values_ref.1, s32[4,64]{1,0:T(4,128)} %bitcast.1), custom_call_target="tpu_custom_call" | custom-call | tf_op jit(solution)/shard_map/pallas_call | solution.py:305
  29.9 0.6 %copy.9 = f32[64,306]{1,0:T(8,128)} copy(f32[64,306]{1,0:T(8,128)S(1)} %get-tuple-element.2) | data formatting | bytes 156672
  30.5 0.6 %copy.10 = f32[64,256]{1,0:T(8,128)} copy(f32[64,256]{1,0:T(8,128)S(1)} %get-tuple-element.3) | data formatting | bytes 131072
